TPU v7x, 32 devices: a whole 2x2x4 slice. The times are simulated.
32 devices in a mesh: seq: 16 (over z, y, x), slide: 2 (over core).
Axes of the slice: x: 2, y: 2, z: 4, core: 2. Of those that a mesh axis runs over, the one named last changes fastest.
Arguments:
- tile_embed: bfloat16 [16384, 768], P(('slide', 'seq')), parts along dimension 0, may hold values from -6 to 6
- valid_tiles: int32 [2], P('slide'), parts along dimension 0, may hold values from 4096 to 8192
- offsets: int32 [16], replicated, may hold values from 0 to 15
- norm_gain: float32 [768], replicated, may hold values from 0.1 to 1.9
- w_qkv: bfloat16 [768, 2304], replicated
- sub_gain: float32 [768], replicated, may hold values from 0.1 to 1.9
- w_out: bfloat16 [768, 768], replicated, may hold values from -0.21875 to 0.21875
Outputs:
- encoded: bfloat16 [16384, 768], P(('slide', 'seq')), parts along dimension 0
There are 2 independent parts, one for each index of `slide`. A program takes and returns all parts, laid end to end along the dimension named above; an argument that names none is the same for every part. Nothing has to cross between parts.
All inputs are finite; a program needn't handle non-finite values.
Results may differ from a plain program's by a relative error of at most 0.0078.
Values may be sent and summed in bfloat16 or wider, within the bound.
A program may use at most 128 MiB of HBM per device.

v0:
```python
import jax
import jax.numpy as jnp
from jax import lax
from jax.sharding import PartitionSpec as P

MIDDLE_DILATION = 4
FAR_DILATION = 16


NEGATIVE = -1e30
EPSILON = 1e-05


def partner_2(value, axis, apart):
    mask = 2**apart
    pairs = [(source, source ^ mask) for source in range(lax.axis_size(axis))]
    return lax.ppermute(value, axis, pairs)


def layer_norm(matrix, gain_row):
    average = jnp.mean(matrix, axis=-1, keepdims=True)
    centred = matrix - average
    variance = jnp.mean(centred * centred, axis=-1, keepdims=True)
    return centred * lax.rsqrt(variance + EPSILON) * gain_row


def attend(packed):
    query_rows, key_rows, value_rows, key_alive = packed
    scores = jnp.dot(query_rows, key_rows.T, preferred_element_type=jnp.float32) * query_rows.shape[
        -1
    ] ** (-0.5)
    scores = jnp.where(key_alive[None, :], scores, NEGATIVE)
    row_max = jnp.max(scores, axis=1)
    weights = jnp.where(key_alive[None, :], jnp.exp(scores - row_max[:, None]), 0.0)
    row_sum = jnp.sum(weights, axis=1)
    numerator = jnp.dot(
        weights.astype(jnp.bfloat16), value_rows, preferred_element_type=jnp.float32
    )
    return (row_max, row_sum, numerator)


def selected_rows(buffer, offsets, dilation):
    dims_now = buffer.shape
    tiled = buffer.reshape(dims_now[:-2] + (dims_now[-2] // dilation, dilation, dims_now[-1]))
    onehot = (
        jnp.arange(dilation, dtype=jnp.int32)[None, :] == (offsets % dilation)[:, None]
    ).astype(buffer.dtype)
    return jnp.einsum(
        "...hnrc,hr->...hnc", tiled, onehot, preferred_element_type=jnp.float32
    ).astype(buffer.dtype)


def flat_selection(key_value_rows, offsets, dilation):
    row_total, pair_count, head_count, head_size = key_value_rows.shape
    if dilation == 1:
        return key_value_rows.transpose(1, 0, 2, 3).reshape(
            pair_count, row_total, head_count * head_size
        )
    tiled = key_value_rows.reshape(
        row_total // dilation, dilation, pair_count, head_count, head_size
    )
    onehot = (
        jnp.arange(dilation, dtype=jnp.int32)[None, :] == (offsets % dilation)[:, None]
    ).astype(key_value_rows.dtype)
    chosen = jnp.einsum("nrkhc,hr->knhc", tiled, onehot, preferred_element_type=jnp.float32).astype(
        key_value_rows.dtype
    )
    return chosen.reshape(pair_count, row_total // dilation, head_count * head_size)


def doubling_round(buffer, bit_count, device_position):
    sections = []
    for bit_index in range(bit_count):
        partner = partner_2(buffer, "seq", bit_index)
        upper_half = device_position >> bit_index & 1 == 1
        buffer = jnp.where(
            upper_half,
            jnp.concatenate([partner, buffer], axis=1),
            jnp.concatenate([buffer, partner], axis=1),
        )
        sections.append(buffer)
    return sections


def branch_terms(
    query_rows,
    keyval,
    offsets,
    valid_tile_count,
    device_position,
    count_of_rows,
    bit_count,
    dilation,
):
    head_count, per_device, head_size = query_rows.shape
    key_count = keyval.shape[1]
    split_keys = keyval.reshape(2, key_count, head_count, head_size).transpose(0, 2, 1, 3)
    chosen_mod = offsets % dilation
    first_row = (device_position >> bit_count << bit_count) * count_of_rows
    positions = (
        first_row + jnp.arange(key_count, dtype=jnp.int32)[None, :] * dilation + chosen_mod[:, None]
    )
    key_alive = positions < valid_tile_count
    row_max, row_sum, numerator = lax.map(
        attend, (query_rows, split_keys[0], split_keys[1], key_alive)
    )
    if dilation == 1:
        return (row_max, row_sum, numerator)
    onehot = jnp.arange(dilation, dtype=jnp.int32)[None, :] == chosen_mod[:, None]
    row_max = jnp.where(onehot[:, None, :], row_max[:, :, None], NEGATIVE).reshape(
        head_count, per_device * dilation
    )
    row_sum = jnp.where(onehot[:, None, :], row_sum[:, :, None], 0.0).reshape(
        head_count, per_device * dilation
    )
    numerator = jnp.where(onehot[:, None, :, None], numerator[:, :, None, :], 0.0).reshape(
        head_count, per_device * dilation, head_size
    )
    return (row_max, row_sum, numerator)


def body(tile_embed, valid_tiles, offsets, norm_gain, w_qkv, sub_gain, w_out):
    devices = lax.axis_size("seq")
    device_position = lax.axis_index("seq")
    count_of_rows, model_width = tile_embed.shape
    head_count = offsets.shape[0]
    head_size = model_width // head_count
    pieces = tile_embed.reshape(devices, count_of_rows // devices, model_width)
    arrived = lax.all_to_all(pieces, "seq", split_axis=0, concat_axis=0, tiled=True)
    relaid = arrived.transpose(1, 0, 2).reshape(count_of_rows, model_width)
    normed = layer_norm(relaid.astype(jnp.float32), norm_gain).astype(jnp.bfloat16)
    projected = jnp.dot(normed, w_qkv, preferred_element_type=jnp.float32).astype(jnp.bfloat16)
    query_rows = (
        projected[:, :model_width].reshape(count_of_rows, head_count, head_size).transpose(1, 0, 2)
    )
    key_value_rows = projected[:, model_width:].reshape(count_of_rows, 2, head_count, head_size)
    valid_tile_count = valid_tiles[0]
    middle_partner_bits = max(4, devices // 16).bit_length() - 1
    distant_partner_bits = max(8, devices // 4).bit_length() - 1
    every_partner_bit = devices.bit_length() - 1
    near_keys = doubling_round(flat_selection(key_value_rows, offsets, 1), 1, device_position)[-1]
    middle_branch_keys = doubling_round(
        flat_selection(key_value_rows, offsets, MIDDLE_DILATION),
        middle_partner_bits,
        device_position,
    )[-1]
    distant_rows = flat_selection(key_value_rows, offsets, FAR_DILATION)
    broad_key_rows = doubling_round(distant_rows, distant_partner_bits, device_position)[-1]
    complete_key_rows = lax.all_gather(distant_rows, "seq", axis=1, tiled=True)
    distant_query_rows = selected_rows(query_rows, offsets, FAR_DILATION)
    branch_list = [
        branch_terms(
            query_rows, near_keys, offsets, valid_tile_count, device_position, count_of_rows, 1, 1
        ),
        branch_terms(
            selected_rows(query_rows, offsets, MIDDLE_DILATION),
            middle_branch_keys,
            offsets,
            valid_tile_count,
            device_position,
            count_of_rows,
            middle_partner_bits,
            MIDDLE_DILATION,
        ),
        branch_terms(
            distant_query_rows,
            broad_key_rows,
            offsets,
            valid_tile_count,
            device_position,
            count_of_rows,
            distant_partner_bits,
            FAR_DILATION,
        ),
        branch_terms(
            distant_query_rows,
            complete_key_rows,
            offsets,
            valid_tile_count,
            device_position,
            count_of_rows,
            every_partner_bit,
            FAR_DILATION,
        ),
    ]
    highest = branch_list[0][0]
    for result in branch_list[1:]:
        highest = jnp.maximum(highest, result[0])
    denom = jnp.zeros_like(highest)
    numer_all = jnp.zeros_like(branch_list[0][2])
    for result in branch_list:
        factor = jnp.exp(result[0] - highest)
        denom = denom + factor * result[1]
        numer_all = numer_all + factor[:, :, None] * result[2]
    attended = (numer_all / jnp.maximum(denom, 1.0)[:, :, None]).astype(jnp.bfloat16)
    flattened = attended.transpose(1, 0, 2).reshape(count_of_rows, model_width)
    sub_normed = layer_norm(flattened.astype(jnp.float32), sub_gain).astype(jnp.bfloat16)
    return (
        relaid.astype(jnp.float32) + jnp.dot(sub_normed, w_out, preferred_element_type=jnp.float32)
    ).astype(jnp.bfloat16)


def solution(mesh):
    return jax.shard_map(
        body,
        mesh=mesh,
        in_specs=(P(("slide", "seq"), None), P("slide"), P(), P(), P(), P(), P()),
        out_specs=P(("slide", "seq"), None),
        check_vma=False,
    )
```

profile of v0, /device:TPU:0, one launch (start us, length us, event | category | flops | bytes accessed | tf_op | source)
XLA Modules:
  0.0 377.6 jit_solution(14723516207113283482)
XLA Ops:
  6.5 8.6 %all-to-all-start = ((bf16[16,32,768]{2,1,0:T(8,128)(2,1)}), bf16[16,32,768]{2,1,0:T(8,128)(2,1)}, u32[]{:S(2)}, u32[]{:S(2)}) async-start(bf16[16,32,768]{2,1,0:T(8,128)(2,1)} %bitcast.294), calls=%async_computation | async-start | bytes 1572864 | tf_op jit(solution)/shard_map/all_to_all | solution.py:129
  24.5 10.5 %all-to-all-done = bf16[16,32,768]{2,1,0:T(8,128)(2,1)} async-done(((bf16[16,32,768]{2,1,0:T(8,128)(2,1)}), bf16[16,32,768]{2,1,0:T(8,128)(2,1)}, u32[]{:S(2)}, u32[]{:S(2)}) %all-to-all-start) | async-done | bytes 786464 | tf_op jit(solution)/shard_map/all_to_all | solution.py:129
  48.7 2.9 copy.243
  53.2 5.2 %reshape_reshape.7 = bf16[32,16,2,16,48]{4,3,2,1,0:T(8,128)(2,1)} reshape(bf16[512,1536]{1,0:T(8,128)(2,1)S(1)} %slice.41) | data formatting | bytes 3145728 | tf_op jit(solution)/shard_map/reshape;reshape | solution.py:59
  58.4 4.7 %fusion.79 = bf16[16,1,32,2,48]{4,1,3,2,0:T(2,128)(2,1)S(1)} fusion(bf16[32,16,2,16,48]{4,3,2,1,0:T(8,128)(2,1)} %reshape_reshape.7, pred[16,16,1,1,1]{1,0,2,3,4:T(8,128)(4,1)S(1)} %copy-done.19), kind=kOutput, calls=%fused_computation.97 | convolution fusion | flops 1572864 | bytes 1671424 | tf_op jit(solution)/shard_map/nrkhc,hr->knhc/dot_general | solution.py:65
  65.3 5.2 %reshape_reshape.6 = bf16[128,4,2,16,48]{4,3,2,1,0:T(8,128)(2,1)} reshape(bf16[512,1536]{1,0:T(8,128)(2,1)S(1)} %slice.41) | data formatting | bytes 3145728 | tf_op jit(solution)/shard_map/reshape;reshape | solution.py:59
  72.0 4.1 %multiply_reduce_fusion = bf16[16,128,2,48]{3,0,2,1:T(8,128)(2,1)S(1)} fusion(f32[16,4]{0,1:T(4,128)S(1)} %copy-done.23, bf16[128,4,2,16,48]{4,3,2,1,0:T(8,128)(2,1)} %reshape_reshape.6), kind=kLoop, calls=%fused_computation.84 | loop fusion | flops 2162688 | bytes 1966336
  86.6 2.2 collective-permute-start.5
  89.9 31.9 %collective-permute-done.1 = bf16[2,128,768]{1,2,0:T(8,128)(2,1)S(1)} collective-permute-done((bf16[2,128,768]{1,2,0:T(8,128)(2,1)}, bf16[2,128,768]{1,2,0:T(8,128)(2,1)S(1)}, u32[]{:S(2)}, u32[]{:S(2)}) %collective-permute-start.1) | collective-permute-done | bytes 393248 | tf_op jit(solution)/shard_map/ppermute | solution.py:17
  127.0 33.4 %while.62 = (s32[]{:T(128)}, f32[16,32]{1,0:T(8,128)S(1)}, f32[16,32]{1,0:T(8,128)S(1)}, f32[16,32,48]{2,1,0:T(8,128)S(1)}, pred[16,256]{1,0:T(8,128)(4,1)}, /*i...) while((s32[]{:T(128)}, f32[16,32]{1,0:T(8,128)S(1)}, ...), condition=%wide.region_13.14_spmd.clone, body=%wide.region_10.13_spmd.sunk.clone | while | flops 1646530 | bytes 177385 | solution.py:104
  163.5 45.2 %while.61 = (s32[]{:T(128)}, f32[16,128]{1,0:T(8,128)S(1)}, f32[16,128]{1,0:T(8,128)S(1)}, f32[16,128,48]{1,2,0:T(8,128)}, pred[16,512]{1,0:T(8,128)(4,1)}, /*in...) while((s32[]{:T(128)}, f32[16,128]{1,0:T(8,128)S(1)}, ...), condition=%wide.region_9.10_spmd.clone, body=%wide.region_6.9_spmd.sunk.clone | while | flops 13172482 | bytes 950889 | solution.py:104
  209.2 2.4 copy.215
  211.5 4.2 %fusion.84 = bf16[2,16,1024,48]{2,3,1,0:T(8,128)(2,1)S(1)} fusion(bf16[2,512,16,48]{1,3,2,0:T(8,128)(2,1)} %bitcast.33, bf16[2,512,16,48]{1,3,2,0:T(8,128)(2,1)} %bitcast.35, pred[]{:T(512)S(6)} %eq.43), kind=kLoop, calls=%fused_computation.106 | loop fusion | flops 14155776 | bytes 6291457 | tf_op jit(solution)/shard_map/transpose | solution.py:97
  215.8 2.3 slice_bitcast_fusion
  218.1 70.1 %while.60 = (s32[]{:T(128)}, f32[16,512]{1,0:T(8,128)S(1)}, f32[16,512]{1,0:T(8,128)S(1)}, f32[16,512,48]{1,2,0:T(8,128)}, pred[16,1024]{1,0:T(8,128)(4,1)S(1)},...) while((s32[]{:T(128)}, f32[16,512]{1,0:T(8,128)S(1)}, ...), condition=%wide.region_5.6_spmd.clone, body=%wide.region_2.5_spmd.sunk.clone | while | flops 107478016 | bytes 6741097 | solution.py:104
  250.9 2.2 fusion.154
  264.0 2.2 fusion.154
  288.2 5.0 %copy.213 = f32[16,512,48]{2,0,1:T(8,128)} copy(f32[16,512,48]{1,2,0:T(8,128)} %get-tuple-element.185) | data formatting | bytes 3145728 | tf_op jit(solution)/shard_map/while | solution.py:104
  295.1 34.0 %while.63 = (s32[]{:T(128)}, f32[16,32]{1,0:T(8,128)S(1)}, f32[16,32]{1,0:T(8,128)S(1)}, f32[16,32,48]{2,1,0:T(8,128)S(1)}, pred[16,512]{1,0:T(8,128)(4,1)}, /*i...) while((s32[]{:T(128)}, f32[16,32]{1,0:T(8,128)S(1)}, ...), condition=%wide.region_17.18_spmd.clone, body=%wide.region_14.17_spmd.sunk.clone | while | flops 3293122 | bytes 325609 | solution.py:104
  336.2 16.1 %convert_reduce_fusion = (f32[512]{0:T(512)S(1)}, bf16[16,512,48]{2,0,1:T(8,128)(2,1)S(1)}) fusion(f32[16,512]{0,1:T(8,128)S(1)} %copy.224, f32[16,512,48]{2,1,0:T(8,128)S(1)} %bitcast.278, f32[16,512]{0,1:T(8,128)S(1)} %copy-done.12, f32[16,512,48]{2,1,0:T(8,128)S(1)} %bitcast.277, pred[16,512]{0,1:T(8,128)(4,1)S(1)} %copy-done.17, ...), kind=kLoop, calls=%fused_computation.86 | loop fusion | flops 5504512 | bytes 6080512 | tf_op jit(solution)/shard_map/reduce_sum | solution.py:21
  352.3 2.3 convert_bitcast_fusion
  354.7 7.4 %fusion.73 = f32[512]{0:T(512)S(1)} fusion(bf16[16,512,48]{2,0,1:T(8,128)(2,1)S(1)} %get-tuple-element.418, f32[512]{0:T(512)S(1)} %broadcast_multiply_fusion.1), kind=kLoop, calls=%fused_computation.90 | loop fusion | flops 1572352 | bytes 790528 | tf_op jit(solution)/shard_map/reduce_sum | solution.py:23
  362.1 3.7 copy.225
  367.7 3.1 fusion.92
  (545 shorter events, 236.0 us)
Async XLA Ops:
  6.5 37.8 %copy-start = (bf16[768,2304]{1,0:T(8,128)(2,1)S(1)}, bf16[768,2304]{1,0:T(8,128)(2,1)}, u32[]{:S(2)}) copy-start(bf16[768,2304]{1,0:T(8,128)(2,1)} %param.19) | copy-start | bytes 10616836
  6.5 28.4 %all-to-all-start = ((bf16[16,32,768]{2,1,0:T(8,128)(2,1)}), bf16[16,32,768]{2,1,0:T(8,128)(2,1)}, u32[]{:S(2)}, u32[]{:S(2)}) async-start(bf16[16,32,768]{2,1,0:T(8,128)(2,1)} %bitcast.294), calls=%async_computation | async-start | bytes 1572864 | tf_op jit(solution)/shard_map/all_to_all | solution.py:129
  15.2 278.0 %all-gather.2.cloned.1.call-start = ((), (), s32[]{:S(2)}) async-start(), calls=%async_computation.1 | async-start | bytes 1671168 | tf_op jit(solution)/shard_map/all_gather | solution.py:149
  53.2 5.2 %copy-start.19 = (pred[16,16,1,1,1]{1,0,2,3,4:T(8,128)(4,1)S(1)}, pred[16,16,1,1,1]{1,0,2,3,4:T(8,128)(4,1)}, u32[]{:S(2)}) copy-start(pred[16,16,1,1,1]{1,0,2,3,4:T(8,128)(4,1)} %get-tuple-element.444) | copy-start | bytes 772
  64.7 7.3 %copy-start.23 = (f32[16,4]{0,1:T(4,128)S(1)}, f32[16,4]{0,1:T(4,128)}, u32[]{:S(2)}) copy-start(f32[16,4]{0,1:T(4,128)} %get-tuple-element.440) | copy-start | bytes 772
  64.7 14.3 %collective-permute-start.3 = (bf16[2,32,768]{2,1,0:T(8,128)(2,1)}, bf16[2,32,768]{2,1,0:T(8,128)(2,1)}, u32[]{:S(2)}, u32[]{:S(2)}) collective-permute-start(bf16[2,32,768]{2,1,0:T(8,128)(2,1)} %copy.244), channel_id=1, source_target_pairs={{0,2},{2,0},{4,6},{6,4},{8,10},{10,8},{12,14},{14,12},{16,18},{18,... | collective-permute-start | bytes 294920 | tf_op jit(solution)/shard_map/ppermute | solution.py:17
  70.5 141.0 %collective-permute-start = (bf16[2,512,768]{1,2,0:T(8,128)(2,1)}, bf16[2,512,768]{1,2,0:T(8,128)(2,1)}, u32[]{:S(2)}, u32[]{:S(2)}) collective-permute-start(bf16[2,512,768]{1,2,0:T(8,128)(2,1)} %bitcast.34), channel_id=1, source_target_pairs={{0,2},{2,0},{4,6},{6,4},{8,10},{10,8},{12,14},{14,12},{16,18},{18,... | collective-permute-start | bytes 4718600 | tf_op jit(solution)/shard_map/ppermute | solution.py:17
  72.0 6.5 %copy-start.3 = (bf16[16,512,48]{2,1,0:T(8,128)(2,1)S(1)}, bf16[16,512,48]{2,1,0:T(8,128)(2,1)}, u32[]{:S(2)}) copy-start(bf16[16,512,48]{2,1,0:T(8,128)(2,1)} %copy.191) | copy-start | bytes 2359300
  72.0 6.5 %copy-start.18 = (pred[16,16,1,1]{1,0,2,3:T(8,128)(4,1)S(1)}, pred[16,16,1,1]{1,0,2,3:T(8,128)(4,1)}, u32[]{:S(2)}) copy-start(pred[16,16,1,1]{1,0,2,3:T(8,128)(4,1)} %get-tuple-element.445) | copy-start | bytes 772
  77.9 3.8 %copy-start.4 = (bf16[16,512,48]{2,0,1:T(8,128)(2,1)S(1)}, bf16[16,512,48]{2,0,1:T(8,128)(2,1)}, u32[]{:S(2)}) copy-start(bf16[16,512,48]{2,0,1:T(8,128)(2,1)} %copy.243) | copy-start | bytes 2359300
  77.9 43.8 %collective-permute-start.1 = (bf16[2,128,768]{1,2,0:T(8,128)(2,1)}, bf16[2,128,768]{1,2,0:T(8,128)(2,1)S(1)}, u32[]{:S(2)}, u32[]{:S(2)}) collective-permute-start(bf16[2,128,768]{1,2,0:T(8,128)(2,1)} %bitcast.284), channel_id=1, source_target_pairs={{0,2},{2,0},{4,6},{6,4},{8,10},{10,8},{12,14},{14,12},{16,18},{18,... | collective-permute-start | bytes 1179656 | tf_op jit(solution)/shard_map/ppermute | solution.py:17
  80.0 5.7 %collective-permute-start.4 = (bf16[2,64,768]{2,1,0:T(8,128)(2,1)S(1)}, bf16[2,64,768]{2,1,0:T(8,128)(2,1)S(1)}, u32[]{:S(2)}, u32[]{:S(2)}) collective-permute-start(bf16[2,64,768]{2,1,0:T(8,128)(2,1)S(1)} %maximum_select_fusion.8), channel_id=1, source_target_pairs={{0,4},{2,6},{4,0},{6,2},{8,12},{10,14},{12,8},{14,10},{16,20},{18,... | collective-permute-start | bytes 589832 | tf_op jit(solution)/shard_map/ppermute | solution.py:17
  84.2 37.6 %copy-start.8 = (bf16[16,128,2,48]{1,3,0,2:T(8,128)(2,1)S(1)}, bf16[16,128,2,48]{1,3,0,2:T(8,128)(2,1)}, u32[]{:S(2)}) copy-start(bf16[16,128,2,48]{1,3,0,2:T(8,128)(2,1)} %copy.237) | copy-start | bytes 1179652
  86.6 38.7 %collective-permute-start.5 = (bf16[2,128,768]{2,1,0:T(8,128)(2,1)}, bf16[2,128,768]{2,1,0:T(8,128)(2,1)}, u32[]{:S(2)}, u32[]{:S(2)}) collective-permute-start(bf16[2,128,768]{2,1,0:T(8,128)(2,1)} %maximum_select_fusion.5), channel_id=1, source_target_pairs={{0,8},{2,10},{4,12},{6,14},{8,0},{10,2},{12,4},{14,6},{16,24},{18,... | collective-permute-start | bytes 1179656 | tf_op jit(solution)/shard_map/ppermute | solution.py:17
  122.9 38.1 %collective-permute-start.2 = (bf16[2,256,768]{1,2,0:T(8,128)(2,1)}, bf16[2,256,768]{1,2,0:T(8,128)(2,1)}, u32[]{:S(2)}, u32[]{:S(2)}) collective-permute-start(bf16[2,256,768]{1,2,0:T(8,128)(2,1)} %maximum_select_fusion.2), channel_id=1, source_target_pairs={{0,4},{2,6},{4,0},{6,2},{8,12},{10,14},{12,8},{14,10},{16,20},{18,... | collective-permute-start | bytes 2359304 | tf_op jit(solution)/shard_map/ppermute | solution.py:17
  160.4 2.4 copy-start.13
  215.8 2.3 copy-start.21
  215.8 2.3 copy-start.22
  295.0 34.6 %copy-start.20 = (pred[16,512]{1,0:T(8,128)(4,1)S(1)}, pred[16,512]{1,0:T(8,128)(4,1)}, u32[]{:S(2)}) copy-start(pred[16,512]{1,0:T(8,128)(4,1)} %copy.198) | copy-start | bytes 24580
  295.1 38.2 %copy-start.14 = (f32[16,32,48]{2,1,0:T(8,128)S(1)}, f32[16,32,48]{2,1,0:T(8,128)}, u32[]{:S(2)}) copy-start(f32[16,32,48]{2,1,0:T(8,128)} %copy-done.13) | copy-start | bytes 294916
  333.6 2.5 copy-start.2
  333.6 2.5 copy-start.9
  362.1 3.7 copy-start.27
  365.8 5.0 %copy-start.1 = (bf16[768,2304]{1,0:T(8,128)(2,1)S(1)}, bf16[768,2304]{1,0:T(8,128)(2,1)}, u32[]{:S(2)}) copy-start(bf16[768,2304]{1,0:T(8,128)(2,1)} %param.19) | copy-start | bytes 10616836
  (13 other events, 17.9 us)
Sparse Core Ops, SparseCore 0:
  64.8 63.7 all-gather.1
where the time goes:
time: 383 us; the launch traced here: 378 us
  matrix products  134 us (35%)
  local copies, waits for them, and re-layouts  97 us (25%)
  other arithmetic  71.5 us (19%)
  waiting for transfers between devices  42.7 us (11%)
  starting transfers between devices  17.3 us (5%)
  between operations  14.7 us (4%)
    dot_general x64, matrix products, attend(): jnp.dot(query_rows, key_rows.T, preferred_element_type=jnp.float32)  69.1 us
    dot_general x64, matrix products, attend(): jnp.dot(weights.astype(jnp.bfloat16), value_rows, preferred_element_type=...  54.3 us
    dynamic_slice x64, local copies, waits for them, and re-layouts, branch_terms(): lax.map(attend, (query_rows, split_keys[0], split_keys[1], key_alive))  34.1 us
    ppermute x6, waiting for transfers between devices, partner_2(): return lax.ppermute(value, axis, pairs)  32.2 us
    reduce_sum x64, other arithmetic, attend(): row_sum = jnp.sum(weights, axis=1)  19.3 us
    reduce_sum x2, other arithmetic, layer_norm(): average = jnp.mean(matrix, axis=-1, keepdims=True)  17.4 us
    another operation x2, local copies, waits for them, and re-layouts, flat_selection(): key_value_rows.reshape(row_total // dilation, dilation, pair_count, head_...  10.5 us
    all_to_all x1, waiting for transfers between devices, body(): lax.all_to_all(pieces, 'seq', split_axis=0, concat_axis=0, tiled=True)  10.5 us
  transfers between devices with their start and end apart: 8, of which 3 were waited for; matrix products, arithmetic and copies ran while one was open for 52% of the time, Pallas kernels for 0%

commit v1 on v0

v1 whole, which is shorter than its diff:
```python
import functools

import jax
import jax.numpy as jnp
import numpy as np
from jax import lax
from jax.experimental import pallas as pl
from jax.experimental.pallas import tpu as pltpu
from jax.sharding import PartitionSpec as P

MIDDLE_DILATION = 4
FAR_DILATION = 16
NEGATIVE = -1e30
EPSILON = 1e-05
LOG2E = 1.4426950408889634
AUG = 16
VMEM_LIMIT = 60 * 1024 * 1024


def layer_norm_rows(x, gain):
    average = jnp.mean(x, axis=-1, keepdims=True)
    centred = x - average
    variance = jnp.mean(centred * centred, axis=-1, keepdims=True)
    return centred * lax.rsqrt(variance + EPSILON) * gain


def project_into(dst, x_ref, gain_ref, w_ref, chunk, skip=0):
    normed = layer_norm_rows(x_ref[...].astype(jnp.float32), gain_ref[...]).astype(jnp.bfloat16)

    @pl.loop(0, (w_ref.shape[0] - skip) // chunk)
    def _(i):
        rows = pl.ds(pl.multiple_of(i * chunk, chunk), chunk)
        dst[rows, :] = lax.dot_general(
            w_ref[pl.ds(pl.multiple_of(i * chunk + skip, chunk), chunk), :], normed, (((1,), (1,)), ((), ())), preferred_element_type=jnp.float32
        ).astype(jnp.bfloat16)


def project_kernel(heads, offs, x_ref, gain_ref, w_ref, proj_ref, mid_ref, far_ref, far_scr):
    rows, width = x_ref.shape
    size = width // heads
    lanes = rows // MIDDLE_DILATION
    few = rows // FAR_DILATION
    project_into(proj_ref, x_ref, gain_ref, w_ref, 256)
    src = lax.broadcasted_iota(jnp.int32, (lanes, lanes), 0)
    dst = lax.broadcasted_iota(jnp.int32, (lanes, lanes), 1)
    for head in range(heads):
        phase = offs[head] % FAR_DILATION
        quarter = phase % MIDDLE_DILATION
        shift = (phase // MIDDLE_DILATION) * few
        pick = ((src == dst + shift) & (dst < few)).astype(jnp.bfloat16)
        for part in range(2):
            base = part * width + head * size
            block = proj_ref[
                width + base : width + base + size,
                pl.ds(pl.multiple_of(quarter * lanes, lanes), lanes),
            ]
            mid_ref[base : base + size, :] = block
            far_scr[base : base + size, :] = jnp.dot(
                block, pick, preferred_element_type=jnp.float32
            )
    far_ref[...] = far_scr[...].T[:few].astype(jnp.bfloat16)


def aug_rows(first, lanes, second=None):
    spot = lax.broadcasted_iota(jnp.int32, (AUG, lanes), 0)
    rows = jnp.where(spot == 0, first, 0.0)
    if second is not None:
        rows = jnp.where(spot == 1, second, rows)
    return rows.astype(jnp.bfloat16)


def weighted_values(value, weight):
    scaled = (value.astype(jnp.float32) * weight).astype(jnp.bfloat16)
    return jnp.concatenate([scaled, aug_rows(weight, value.shape[1])], axis=0)


def scores_of(keys, queries):
    return lax.dot_general(
        keys, queries, (((0,), (0,)), ((), ())), preferred_element_type=jnp.float32
    )


def own_kernel(scale, per_step, size, valid, q_ref, k_ref, v_ref, pos_ref, out_ref):
    lanes = q_ref.shape[1]
    alive = pos_ref[...] + lax.axis_index("seq") * lanes < valid[0]
    bias = aug_rows(jnp.where(alive, 0.0, NEGATIVE), lanes)
    weight = jnp.where(alive, 1.0, 0.0)
    unit = aug_rows(jnp.ones((1, lanes), jnp.float32), lanes)
    for i in range(per_step):
        part = slice(i * size, (i + 1) * size)
        scores = scores_of(
            jnp.concatenate([k_ref[part, :], bias], axis=0),
            jnp.concatenate([q_ref[part, :], unit], axis=0),
        )
        top = jnp.max(scores, axis=0, keepdims=True)
        p = jnp.exp2((scores - top) * scale).astype(jnp.bfloat16)
        base = i * (size + AUG)
        out_ref[base : base + size + AUG, :] = jnp.dot(
            weighted_values(v_ref[part, :], weight), p, preferred_element_type=jnp.float32
        )
        out_ref[base + size + 1 : base + size + 2, :] = top


def rest_kernel(
    heads, scale, per_step, far_span, middle, offs, valid,
    x_ref, xp_ref, gain_ref, w_ref, q_ref, k_ref, v_ref, own_ref, ppos_ref,
    *rest,
):
    others = middle - 2
    midk, midv = rest[:others], rest[others : 2 * others]
    far_ref, extra_ref, subgain_ref, wout_ref, out_ref, kvp, far_t, o_scr, att = rest[2 * others :]
    rows, width = x_ref.shape
    size = width // heads
    lanes = rows // MIDDLE_DILATION
    few = rows // FAR_DILATION
    step = pl.program_id(0)

    @pl.when(step == 0)
    def _():
        project_into(kvp, xp_ref, gain_ref, w_ref, 256, width)
        for i in range(far_ref.shape[0] // 128):
            far_t[:, i * 128 : (i + 1) * 128] = far_ref[i * 128 : (i + 1) * 128, :].T

    me = lax.axis_index("seq")
    alive = ppos_ref[...] + (me ^ 1) * rows < valid[0]
    bias = aug_rows(jnp.where(alive, 0.0, NEGATIVE), rows)
    weight = jnp.where(alive, 1.0, 0.0)
    unit = aug_rows(jnp.ones((1, rows), jnp.float32), rows)
    is_far = extra_ref[1:2, :]
    device = jnp.where(is_far == 1, extra_ref[2:3, :], extra_ref[2:3, :] ^ me)
    start = extra_ref[0:1, :] + device * rows
    times = jnp.where((is_far == 1) & (extra_ref[3:4, :] == me // far_span), 2, 1)
    lane = lax.broadcasted_iota(jnp.int32, (1, lanes), 1)
    for i in range(per_step):
        head = step * per_step + i
        part = slice(i * size, (i + 1) * size)
        base = i * (size + AUG)
        both = slice(base, base + size + AUG)
        phase = offs[head] % FAR_DILATION
        quarter = phase % MIDDLE_DILATION
        cols = pl.ds(pl.multiple_of(quarter * lanes, lanes), lanes)
        krows = pl.ds(pl.multiple_of(head * size, AUG), size)
        vrows = pl.ds(pl.multiple_of(width + head * size, AUG), size)

        scores = scores_of(
            jnp.concatenate([kvp[krows, :], bias], axis=0),
            jnp.concatenate([q_ref[part, :], unit], axis=0),
        )
        own = own_ref[both, :]
        own_top = own[size + 1 : size + 2, :]
        top = jnp.maximum(own_top, jnp.max(scores, axis=0, keepdims=True))
        p = jnp.exp2((scores - top) * scale).astype(jnp.bfloat16)
        o_scr[both, :] = own * jnp.exp2((own_top - top) * scale) + jnp.dot(
            weighted_values(kvp[vrows, :], weight), p, preferred_element_type=jnp.float32
        )
        o_scr[base + size + 1 : base + size + 2, :] = top

        keys = jnp.concatenate(
            [k_ref[part, cols], kvp[krows, cols]]
            + [midk[g][part, :] for g in range(others)]
            + [far_t[krows, :]],
            axis=1,
        )
        values = jnp.concatenate(
            [v_ref[part, cols], kvp[vrows, cols]]
            + [midv[g][part, :] for g in range(others)]
            + [far_t[vrows, :]],
            axis=1,
        )
        spot = start + jnp.where(is_far == 1, phase, quarter)
        live = spot < valid[0]
        count = jnp.where(live, times, 0).astype(jnp.float32)
        keys = jnp.concatenate(
            [
                keys,
                aug_rows(
                    jnp.where(live, 0.0, NEGATIVE), keys.shape[1], is_far.astype(jnp.float32)
                ),
            ],
            axis=0,
        )
        mine = lane // few == phase // MIDDLE_DILATION
        queries = jnp.concatenate(
            [
                q_ref[part, cols],
                aug_rows(
                    jnp.ones((1, lanes), jnp.float32), lanes, jnp.where(mine, 0.0, NEGATIVE)
                ),
            ],
            axis=0,
        )
        more = scores_of(keys, queries)
        had = o_scr[both, cols]
        had_top = had[size + 1 : size + 2, :]
        new_top = jnp.maximum(had_top, jnp.max(more, axis=0, keepdims=True))
        p = jnp.exp2((more - new_top) * scale).astype(jnp.bfloat16)
        total = had * jnp.exp2((had_top - new_top) * scale) + jnp.dot(
            weighted_values(values, count), p, preferred_element_type=jnp.float32
        )
        o_scr[both, cols] = jnp.where(new_top > 0.5 * NEGATIVE, total, 0.0)
        done = o_scr[both, :]
        result = done[:size] / jnp.maximum(done[size : size + 1], 1.0)
        att[pl.ds(pl.multiple_of(head * size, AUG), size), :] = result.astype(jnp.bfloat16)

    @pl.when(step == pl.num_programs(0) - 1)
    def _():
        attended = att[...].astype(jnp.float32)
        average = jnp.mean(attended, axis=0, keepdims=True)
        centred = attended - average
        variance = jnp.mean(centred * centred, axis=0, keepdims=True)
        normed = centred * lax.rsqrt(variance + EPSILON) * subgain_ref[...]
        projected = jnp.dot(
            normed.T.astype(jnp.bfloat16), wout_ref[...], preferred_element_type=jnp.float32
        )
        out_ref[...] = (x_ref[...].astype(jnp.float32) + projected).astype(jnp.bfloat16)


def body(tile_embed, valid_tiles, offsets, norm_gain, w_qkv, sub_gain, w_out):
    devices = lax.axis_size("seq")
    me = lax.axis_index("seq")
    rows, width = tile_embed.shape
    heads = offsets.shape[0]
    size = width // heads
    lanes = rows // MIDDLE_DILATION
    few = rows // FAR_DILATION
    each = rows // devices
    middle = max(4, devices // 16)
    far_span = max(8, devices // 4)
    per_step = 2
    steps = heads // per_step
    scale = float(size) ** -0.5 * LOG2E

    w_t = w_qkv.T
    pieces = tile_embed.reshape(devices, each, width)
    arrived = lax.all_to_all(pieces, "seq", split_axis=0, concat_axis=0, tiled=True)
    groups = devices // FAR_DILATION
    x = arrived.reshape(groups, 4, 4, each, width).transpose(2, 1, 0, 3, 4).reshape(rows, width)
    xp = lax.ppermute(x, "seq", [(d, d ^ 1) for d in range(devices)])

    whole = lambda *shape: pl.BlockSpec(shape, lambda *_: (0,) * len(shape))
    smem = pl.BlockSpec(memory_space=pltpu.SMEM)
    gain = norm_gain.reshape(1, width)

    proj, mid, far = pl.pallas_call(
        functools.partial(project_kernel, heads),
        out_shape=(
            jax.ShapeDtypeStruct((3 * width, rows), jnp.bfloat16),
            jax.ShapeDtypeStruct((2 * width, lanes), jnp.bfloat16),
            jax.ShapeDtypeStruct((few, 2 * width), jnp.bfloat16),
        ),
        in_specs=[smem] + [pl.BlockSpec(memory_space=pltpu.VMEM)] * 3,
        out_specs=(pl.BlockSpec(memory_space=pltpu.VMEM),) * 3,
        scratch_shapes=[pltpu.VMEM((2 * width, lanes), jnp.float32)],
        compiler_params=pltpu.CompilerParams(vmem_limit_bytes=VMEM_LIMIT),
        cost_estimate=pl.CostEstimate(
            flops=6 * rows * width * width, bytes_accessed=12 * width * width, transcendentals=0
        ),
        name="project",
    )(offsets, x, gain, w_t)

    mids = [
        lax.ppermute(mid, "seq", [(d, d ^ g) for d in range(devices)]) for g in range(2, middle)
    ]
    far_all = lax.all_gather(far, "seq", axis=0, tiled=True)

    local = np.arange(rows, dtype=np.int32).reshape(each, groups, 4, 4).transpose(3, 2, 1, 0)
    local = local.reshape(1, rows)
    seats = np.arange(devices, dtype=np.int32)
    mid_rows = [np.tile(local[0, :lanes], middle), np.zeros(middle * lanes, np.int32),
                np.repeat(np.arange(middle, dtype=np.int32), lanes),
                np.zeros(middle * lanes, np.int32)]
    far_rows = [np.tile(local[0, :few], devices), np.ones(devices * few, np.int32),
                np.repeat(seats, few), np.repeat(seats // far_span, few)]
    extra = np.concatenate([np.stack(mid_rows), np.stack(far_rows)], axis=1)
    extra_count = extra.shape[1]

    strip = per_step * size
    out_strip = per_step * (size + AUG)
    block = lambda part: pl.BlockSpec((strip, rows), lambda h: (part * steps + h, 0))
    own = pl.pallas_call(
        functools.partial(own_kernel, scale, per_step, size),
        grid=(steps,),
        out_shape=jax.ShapeDtypeStruct((heads * (size + AUG), rows), jnp.float32),
        in_specs=[smem, block(0), block(1), block(2), whole(1, rows)],
        out_specs=pl.BlockSpec((out_strip, rows), lambda h: (h, 0)),
        compiler_params=pltpu.CompilerParams(vmem_limit_bytes=VMEM_LIMIT),
        cost_estimate=pl.CostEstimate(
            flops=16 * rows * rows * width, bytes_accessed=8 * rows * width,
            transcendentals=heads * rows * rows,
        ),
        name="own_keys",
    )(valid_tiles, proj, proj, proj, jnp.asarray(local))

    out = pl.pallas_call(
        functools.partial(rest_kernel, heads, scale, per_step, far_span, middle),
        grid=(steps,),
        out_shape=jax.ShapeDtypeStruct((rows, width), jnp.bfloat16),
        in_specs=[
            smem, smem,
            whole(rows, width), whole(rows, width), whole(1, width), whole(3 * width, width),
            block(0), block(1), block(2),
            pl.BlockSpec((out_strip, rows), lambda h: (h, 0)),
            whole(1, rows),
            *[pl.BlockSpec((strip, lanes), lambda h: (h, 0))] * len(mids),
            *[pl.BlockSpec((strip, lanes), lambda h: (steps + h, 0))] * len(mids),
            whole(devices * few, 2 * width), whole(4, extra_count),
            whole(width, 1), whole(width, width),
        ],
        out_specs=whole(rows, width),
        scratch_shapes=[
            pltpu.VMEM((2 * width, rows), jnp.bfloat16),
            pltpu.VMEM((2 * width, devices * few), jnp.bfloat16),
            pltpu.VMEM((out_strip, rows), jnp.float32),
            pltpu.VMEM((width, rows), jnp.bfloat16),
        ],
        compiler_params=pltpu.CompilerParams(vmem_limit_bytes=VMEM_LIMIT),
        cost_estimate=pl.CostEstimate(
            flops=24 * rows * rows * width, bytes_accessed=20 * rows * width,
            transcendentals=heads * rows * rows,
        ),
        name="rest",
    )(
        offsets, valid_tiles, x, xp, gain, w_t, proj, proj, proj, own, jnp.asarray(local),
        *mids, *mids, far_all, jnp.asarray(extra), sub_gain.reshape(width, 1), w_out,
    )
    return (
        out.reshape(4, 4, groups, each, width).transpose(3, 2, 1, 0, 4).reshape(rows, width)
    )


def solution(mesh):
    return jax.shard_map(
        body,
        mesh=mesh,
        in_specs=(P(("slide", "seq"), None), P("slide"), P(), P(), P(), P(), P()),
        out_specs=P(("slide", "seq"), None),
        check_vma=False,
    )
```

time: 383 us -> 137 us (0.36); the launches traced: 378 us -> 136 us
  matrix products: 134 us -> 0 us
  local copies, waits for them, and re-layouts: 97 us -> 11.7 us
  other arithmetic: 71.5 us -> 0 us
  Pallas kernels: 0 us -> 44 us
  waiting for transfers between devices: 42.7 us -> 54.4 us
  starting transfers between devices: 17.3 us -> 11.9 us
    dot_general x132 -> x0, matrix products: 134 us -> none  [the longest x64 69.1 us: attend(): jnp.dot(query_rows, key_rows.T, preferred_element_type=jnp.float32)]
    reduce_sum x68 -> x0, other arithmetic: 45.6 us -> none  [the longest x64 19.3 us: attend(): row_sum = jnp.sum(weights, axis=1)]
    pallas_call x0 -> x3, Pallas kernels: none -> 44 us  [the longest x1 25.1 us: body(): pl.pallas_call(functools.partial(rest_kernel, heads, scale, per_step, far...]
    dynamic_slice x64 -> x0, local copies, waits for them, and re-layouts: 34.1 us -> none  [branch_terms(): lax.map(attend, (query_rows, split_keys[0], split_keys[1], key_alive))]
    all_gather x1, waiting for transfers between devices: 0.01 us -> 30 us  [body(): far_all = lax.all_gather(far, 'seq', axis=0, tiled=True)]
    ppermute x6 -> x3, waiting for transfers between devices: 32.2 us -> 11.8 us  [the longest x2 11.8 us: body(): lax.ppermute(mid, 'seq', [(d, d ^ g) for d in range(devices)])]
    another operation x8 -> x0, local copies, waits for them, and re-layouts: 10.5 us -> none  [the longest x2 10.5 us: flat_selection(): key_value_rows.reshape(row_total // dilation, dilation, pair_count, head_...]
    while x5 -> x0, local copies, waits for them, and re-layouts: 9.32 us -> none  [branch_terms(): lax.map(attend, (query_rows, split_keys[0], split_keys[1], key_alive))]
  transfers between devices with their start and end apart: 8 -> 5, of which waited for: 3 -> 3; matrix products, arithmetic and copies ran while one was open for 52% -> 6% of each run, Pallas kernels for 0% -> 8%
where the time goes in v1:
time: 137 us; the launch traced here: 136 us
  waiting for transfers between devices  54.4 us (40%)
  Pallas kernels  44 us (32%)
  between operations  14.1 us (10%)
  starting transfers between devices  11.9 us (9%)
  local copies, waits for them, and re-layouts  11.7 us (9%)
    all_gather x1, waiting for transfers between devices, body(): far_all = lax.all_gather(far, 'seq', axis=0, tiled=True)  30 us
    pallas_call x1, Pallas kernels, body(): pl.pallas_call(functools.partial(rest_kernel, heads, scale, per_step, far...  25.1 us
    all_to_all x1, waiting for transfers between devices, body(): lax.all_to_all(pieces, 'seq', split_axis=0, concat_axis=0, tiled=True)  12.6 us
    ppermute x2, waiting for transfers between devices, body(): lax.ppermute(mid, 'seq', [(d, d ^ g) for d in range(devices)])  11.8 us
    pallas_call x1, Pallas kernels, body(): pl.pallas_call(functools.partial(own_kernel, scale, per_step, size), grid...  10.7 us
    all_to_all x1, starting transfers between devices, body(): lax.all_to_all(pieces, 'seq', split_axis=0, concat_axis=0, tiled=True)  8.34 us
    pallas_call x1, Pallas kernels, body(): pl.pallas_call(functools.partial(project_kernel, heads), out_shape=(jax.S...  8.23 us
    unnamed x11, local copies, waits for them, and re-layouts  5.78 us
  transfers between devices with their start and end apart: 5, of which 3 were waited for; matrix products, arithmetic and copies ran while one was open for 6% of the time, Pallas kernels for 8%

profile of v1, /device:TPU:0, one launch (start us, length us, event | category | flops | bytes accessed | tf_op | source)
XLA Modules:
  0.0 136.2 jit_solution(3368609836367295455)
XLA Ops:
  6.5 8.3 %all-to-all-start = ((bf16[16,32,768]{2,1,0:T(8,128)(2,1)}), bf16[16,32,768]{2,1,0:T(8,128)(2,1)S(1)}, u32[]{:S(2)}, u32[]{:S(2)}) async-start(bf16[16,32,768]{2,1,0:T(8,128)(2,1)} %bitcast.18), calls=%async_computation | async-start | bytes 1572864 | tf_op jit(solution)/shard_map/all_to_all | solution.py:235
  14.9 0.0 all-gather.2.cloned.1.call-start
  14.9 1.3 reshape.24.gain_ref
  16.2 5.8 %copy.13 = bf16[768,2304]{0,1:T(8,128)(2,1)} copy(bf16[768,2304]{1,0:T(8,128)(2,1)} %param.13) | data formatting | bytes 7077888 | tf_op args[4]
  22.0 12.6 %all-to-all-done = bf16[16,32,768]{2,1,0:T(8,128)(2,1)S(1)} async-done(((bf16[16,32,768]{2,1,0:T(8,128)(2,1)}), bf16[16,32,768]{2,1,0:T(8,128)(2,1)S(1)}, u32[]{:S(2)}, u32[]{:S(2)}) %all-to-all-start) | async-done | bytes 786464 | tf_op jit(solution)/shard_map/all_to_all | solution.py:235
  34.6 0.9 copy.12
  35.5 8.2 %project.1 = (bf16[2304,512]{1,0:T(8,128)(2,1)}, bf16[1536,128]{1,0:T(8,128)(2,1)}, bf16[32,1536]{1,0:T(8,128)(2,1)}) custom-call(s32[16]{0:T(128)} %offs.3, bf16[512,768]{1,0:T(8,128)(2,1)} %bitcast.13, f32[1,768]{1,0:T(1,128)} %reshape.24.gain_ref, bf16[2304,768]{1,0:T(8,128)(2,1)} %bitcast.11), custom_call_target="tpu_custom_call" | custom-call | flops 1811939328 | bytes 7077888 | tf_op jit(solution)/shard_map/project/pallas_call | solution.py:244
  43.8 0.0 all-gather.2.cloned.1.call-update
  43.8 0.0 copy-done
  43.8 0.6 collective-permute-start
  44.4 2.5 %collective-permute-start.2 = (bf16[1536,128]{1,0:T(8,128)(2,1)}, bf16[1536,128]{1,0:T(8,128)(2,1)S(1)}, u32[]{:S(2)}, u32[]{:S(2)}) collective-permute-start(bf16[1536,128]{1,0:T(8,128)(2,1)} %get-tuple-element.9), channel_id=1, source_target_pairs={{0,6},{2,4},{4,2},{6,0},{8,14},{10,12},{12,10},{14,8},{16,22},{18,... | collective-permute-start | bytes 1179656 | tf_op jit(solution)/shard_map/ppermute | solution.py:262
  46.9 0.4 collective-permute-start.1
  48.0 0.0 copy-done.4
  48.0 0.9 reshape.28.rest_6_
  48.9 10.7 %own_keys.1.own_ref = f32[1024,512]{1,0:T(8,128)} custom-call(s32[1]{0:T(128)S(6)} %copy.16.valid, bf16[2304,512]{1,0:T(8,128)(2,1)} %get-tuple-element.8.q_ref.k_ref.v_ref, bf16[2304,512]{1,0:T(8,128)(2,1)} %get-tuple-element.8.q_ref.k_ref.v_ref, bf16[2304,512]{1,0:T(8,128)(2,1)} %get-tuple-element.8.q_ref.k_ref.v_ref, s32[1,512]{1,0:T(1,128)} %constant.4.clone.pos_ref.ppos_ref), custom_call_target="tpu_custom_call" | custom-call | flops 3221225472 | bytes 3145728 | tf_op jit(solution)/shard_map/own_keys/pallas_call | solution.py:280
  59.6 11.8 %collective-permute-done.2.rest_1_.rest_3_ = bf16[1536,128]{1,0:T(8,128)(2,1)S(1)} collective-permute-done((bf16[1536,128]{1,0:T(8,128)(2,1)}, bf16[1536,128]{1,0:T(8,128)(2,1)S(1)}, u32[]{:S(2)}, u32[]{:S(2)}) %collective-permute-start.2) | collective-permute-done | bytes 393248 | tf_op jit(solution)/shard_map/ppermute | solution.py:262
  71.4 0.0 collective-permute-done.1.rest_0_.rest_2_
  71.4 0.0 collective-permute-done.xp_ref
  71.4 0.0 copy-start.3
  71.4 30.0 %all-gather.2.cloned.1.call-done.rest_4_ = bf16[512,1536]{1,0:T(8,128)(2,1)} async-done(((bf16[32,1536]{1,0:T(8,128)(2,1)}), bf16[512,1536]{1,0:T(8,128)(2,1)}) %all-gather.2.cloned.1.call-update) | async-done | bytes 1572880 | tf_op jit(solution)/shard_map/all_gather | solution.py:264
  101.4 0.0 copy-done.2
  101.4 25.1 %rest.1 = bf16[512,768]{1,0:T(8,128)(2,1)} custom-call(s32[16]{0:T(128)} %offs.3, s32[1]{0:T(128)S(6)} %copy.16.valid, bf16[512,768]{1,0:T(8,128)(2,1)} %bitcast.14, bf16[512,768]{1,0:T(8,128)(2,1)} %copy-done.3, f32[1,768]{1,0:T(1,128)} %reshape.24.gain_ref, bf16[2304,768]{1,0:T(8,128)(2,1)} %bitcast.12, ...), custom_call_target="tpu_custom_call" | custom-call | flops 4831838208 | bytes 7864320 | tf_op jit(solution)/shard_map/rest/pallas_call | solution.py:294
  126.5 1.7 %copy.15 = bf16[32,1,4,4,768]{4,3,2,0,1:T(4,128)(2,1)S(1)} copy(bf16[32,1,4,4,768]{4,0,2,3,1:T(8,128)(2,1)} %bitcast.16) | data formatting | bytes 1572864 | tf_op jit(solution)/shard_map/transpose | solution.py:327
  128.3 1.1 reshape.27
  (6 shorter events, 0.0 us)
Async XLA Ops:
  6.5 28.0 %all-to-all-start = ((bf16[16,32,768]{2,1,0:T(8,128)(2,1)}), bf16[16,32,768]{2,1,0:T(8,128)(2,1)S(1)}, u32[]{:S(2)}, u32[]{:S(2)}) async-start(bf16[16,32,768]{2,1,0:T(8,128)(2,1)} %bitcast.18), calls=%async_computation | async-start | bytes 1572864 | tf_op jit(solution)/shard_map/all_to_all | solution.py:235
  14.9 86.6 %all-gather.2.cloned.1.call-start = ((), (), s32[]{:S(2)}) async-start(), calls=%async_computation.1 | async-start | bytes 1671168 | tf_op jit(solution)/shard_map/all_gather | solution.py:264
  35.5 8.3 %copy-start = (bf16[4,4,1,32,768]{4,3,1,0,2:T(8,128)(2,1)S(1)}, bf16[4,4,1,32,768]{4,3,1,0,2:T(8,128)(2,1)}, u32[]{:S(2)}) copy-start(bf16[4,4,1,32,768]{4,3,1,0,2:T(8,128)(2,1)} %copy.12) | copy-start | bytes 2359300
  35.5 12.5 %copy-start.4 = (f32[768]{0:T(1024)S(1)}, f32[768]{0:T(1024)}, u32[]{:S(2)}) copy-start(f32[768]{0:T(1024)} %param.14) | copy-start | bytes 9220
  43.8 27.6 %collective-permute-start = (bf16[512,768]{1,0:T(8,128)(2,1)S(1)}, bf16[512,768]{1,0:T(8,128)(2,1)S(1)}, u32[]{:S(2)}, u32[]{:S(2)}) collective-permute-start(bf16[512,768]{1,0:T(8,128)(2,1)S(1)} %bitcast.15), channel_id=1, source_target_pairs={{0,2},{2,0},{4,6},{6,4},{8,10},{10,8},{12,14},{14,12},{16,18},{18,... | collective-permute-start | bytes 2359304 | tf_op jit(solution)/shard_map/ppermute | solution.py:238
  44.4 27.0 %collective-permute-start.2 = (bf16[1536,128]{1,0:T(8,128)(2,1)}, bf16[1536,128]{1,0:T(8,128)(2,1)S(1)}, u32[]{:S(2)}, u32[]{:S(2)}) collective-permute-start(bf16[1536,128]{1,0:T(8,128)(2,1)} %get-tuple-element.9), channel_id=1, source_target_pairs={{0,6},{2,4},{4,2},{6,0},{8,14},{10,12},{12,10},{14,8},{16,22},{18,... | collective-permute-start | bytes 1179656 | tf_op jit(solution)/shard_map/ppermute | solution.py:262
  46.9 24.5 %collective-permute-start.1 = (bf16[1536,128]{1,0:T(8,128)(2,1)}, bf16[1536,128]{1,0:T(8,128)(2,1)S(1)}, u32[]{:S(2)}, u32[]{:S(2)}) collective-permute-start(bf16[1536,128]{1,0:T(8,128)(2,1)} %get-tuple-element.9), channel_id=1, source_target_pairs={{0,4},{2,6},{4,0},{6,2},{8,12},{10,14},{12,8},{14,10},{16,20},{18,... | collective-permute-start | bytes 1179656 | tf_op jit(solution)/shard_map/ppermute | solution.py:262
  71.4 30.1 %copy-start.1 = (bf16[1536,128]{1,0:T(8,128)(2,1)}, bf16[1536,128]{1,0:T(8,128)(2,1)S(1)}, u32[]{:S(2)}) copy-start(bf16[1536,128]{1,0:T(8,128)(2,1)S(1)} %collective-permute-done.2.rest_1_.rest_3_) | copy-start | bytes 1179652
  71.4 30.0 %copy-start.2 = (bf16[1536,128]{1,0:T(8,128)(2,1)}, bf16[1536,128]{1,0:T(8,128)(2,1)S(1)}, u32[]{:S(2)}) copy-start(bf16[1536,128]{1,0:T(8,128)(2,1)S(1)} %collective-permute-done.1.rest_0_.rest_2_) | copy-start | bytes 1179652
  71.4 30.0 %copy-start.3 = (bf16[512,768]{1,0:T(8,128)(2,1)}, bf16[512,768]{1,0:T(8,128)(2,1)S(1)}, u32[]{:S(2)}) copy-start(bf16[512,768]{1,0:T(8,128)(2,1)S(1)} %collective-permute-done.xp_ref) | copy-start | bytes 2359300
Sparse Core Ops, SparseCore 0:
  43.9 57.4 all-gather.1

commit v2 on v1

--- a/solution.py
+++ b/solution.py
@@ -35,7 +35,7 @@
         ).astype(jnp.bfloat16)
 
 
-def project_kernel(heads, offs, x_ref, gain_ref, w_ref, proj_ref, mid_ref, far_ref, far_scr):
+def project_kernel(heads, offs, x_ref, gain_ref, w_ref, proj_ref, mid_ref, fark_ref, farv_ref, far_scr):
     rows, width = x_ref.shape
     size = width // heads
     lanes = rows // MIDDLE_DILATION
@@ -58,7 +58,8 @@
             far_scr[base : base + size, :] = jnp.dot(
                 block, pick, preferred_element_type=jnp.float32
             )
-    far_ref[...] = far_scr[...].T[:few].astype(jnp.bfloat16)
+    fark_ref[...] = far_scr[:width, :].T[:few].astype(jnp.bfloat16)
+    farv_ref[...] = far_scr[width:, :].T[:few].astype(jnp.bfloat16)
 
 
 def aug_rows(first, lanes, second=None):
@@ -108,7 +109,8 @@
 ):
     others = middle - 2
     midk, midv = rest[:others], rest[others : 2 * others]
-    far_ref, extra_ref, subgain_ref, wout_ref, out_ref, kvp, far_t, o_scr, att = rest[2 * others :]
+    fark_ref, farv_ref, extra_ref, subgain_ref, wout_ref = rest[2 * others : 2 * others + 5]
+    out_ref, kvp, far_t, o_scr, att = rest[2 * others + 5 :]
     rows, width = x_ref.shape
     size = width // heads
     lanes = rows // MIDDLE_DILATION
@@ -118,8 +120,9 @@
     @pl.when(step == 0)
     def _():
         project_into(kvp, xp_ref, gain_ref, w_ref, 256, width)
-        for i in range(far_ref.shape[0] // 128):
-            far_t[:, i * 128 : (i + 1) * 128] = far_ref[i * 128 : (i + 1) * 128, :].T
+        for i in range(fark_ref.shape[0] // 128):
+            far_t[:width, i * 128 : (i + 1) * 128] = fark_ref[i * 128 : (i + 1) * 128, :].T
+            far_t[width:, i * 128 : (i + 1) * 128] = farv_ref[i * 128 : (i + 1) * 128, :].T
 
     me = lax.axis_index("seq")
     alive = ppos_ref[...] + (me ^ 1) * rows < valid[0]
@@ -127,9 +130,9 @@
     weight = jnp.where(alive, 1.0, 0.0)
     unit = aug_rows(jnp.ones((1, rows), jnp.float32), rows)
     is_far = extra_ref[1:2, :]
-    device = jnp.where(is_far == 1, extra_ref[2:3, :], extra_ref[2:3, :] ^ me)
+    device = extra_ref[2:3, :] ^ me
     start = extra_ref[0:1, :] + device * rows
-    times = jnp.where((is_far == 1) & (extra_ref[3:4, :] == me // far_span), 2, 1)
+    times = jnp.where((is_far == 1) & (device // far_span == me // far_span), 2, 1)
     lane = lax.broadcasted_iota(jnp.int32, (1, lanes), 1)
     for i in range(per_step):
         head = step * per_step + i
@@ -213,6 +216,11 @@
             normed.T.astype(jnp.bfloat16), wout_ref[...], preferred_element_type=jnp.float32
         )
         out_ref[...] = (x_ref[...].astype(jnp.float32) + projected).astype(jnp.bfloat16)
+
+
+def doubled(rows, bit, devices):
+    pairs = [(d, d ^ (1 << bit)) for d in range(devices)]
+    return jnp.concatenate([rows, lax.ppermute(rows, "seq", pairs)], axis=0)
 
 
 def body(tile_embed, valid_tiles, offsets, norm_gain, w_qkv, sub_gain, w_out):
@@ -241,15 +249,16 @@
     smem = pl.BlockSpec(memory_space=pltpu.SMEM)
     gain = norm_gain.reshape(1, width)
 
-    proj, mid, far = pl.pallas_call(
+    proj, mid, far_key, far_value = pl.pallas_call(
         functools.partial(project_kernel, heads),
         out_shape=(
             jax.ShapeDtypeStruct((3 * width, rows), jnp.bfloat16),
             jax.ShapeDtypeStruct((2 * width, lanes), jnp.bfloat16),
-            jax.ShapeDtypeStruct((few, 2 * width), jnp.bfloat16),
+            jax.ShapeDtypeStruct((few, width), jnp.bfloat16),
+            jax.ShapeDtypeStruct((few, width), jnp.bfloat16),
         ),
         in_specs=[smem] + [pl.BlockSpec(memory_space=pltpu.VMEM)] * 3,
-        out_specs=(pl.BlockSpec(memory_space=pltpu.VMEM),) * 3,
+        out_specs=(pl.BlockSpec(memory_space=pltpu.VMEM),) * 4,
         scratch_shapes=[pltpu.VMEM((2 * width, lanes), jnp.float32)],
         compiler_params=pltpu.CompilerParams(vmem_limit_bytes=VMEM_LIMIT),
         cost_estimate=pl.CostEstimate(
@@ -261,16 +270,23 @@
     mids = [
         lax.ppermute(mid, "seq", [(d, d ^ g) for d in range(devices)]) for g in range(2, middle)
     ]
-    far_all = lax.all_gather(far, "seq", axis=0, tiled=True)
+    bits = devices.bit_length() - 1
+    for bit in range(bits):
+        far_key = doubled(far_key, bit, devices)
+        far_value = doubled(far_value, bits - 1 - bit, devices)
+    far_value = (
+        far_value.reshape((2,) * bits + (few, width))
+        .transpose(tuple(reversed(range(bits))) + (bits, bits + 1))
+        .reshape(devices * few, width)
+    )
 
     local = np.arange(rows, dtype=np.int32).reshape(each, groups, 4, 4).transpose(3, 2, 1, 0)
     local = local.reshape(1, rows)
     seats = np.arange(devices, dtype=np.int32)
     mid_rows = [np.tile(local[0, :lanes], middle), np.zeros(middle * lanes, np.int32),
-                np.repeat(np.arange(middle, dtype=np.int32), lanes),
-                np.zeros(middle * lanes, np.int32)]
+                np.repeat(np.arange(middle, dtype=np.int32), lanes)]
     far_rows = [np.tile(local[0, :few], devices), np.ones(devices * few, np.int32),
-                np.repeat(seats, few), np.repeat(seats // far_span, few)]
+                np.repeat(seats, few)]
     extra = np.concatenate([np.stack(mid_rows), np.stack(far_rows)], axis=1)
     extra_count = extra.shape[1]
 
@@ -303,7 +319,7 @@
             whole(1, rows),
             *[pl.BlockSpec((strip, lanes), lambda h: (h, 0))] * len(mids),
             *[pl.BlockSpec((strip, lanes), lambda h: (steps + h, 0))] * len(mids),
-            whole(devices * few, 2 * width), whole(4, extra_count),
+            whole(devices * few, width), whole(devices * few, width), whole(3, extra_count),
             whole(width, 1), whole(width, width),
         ],
         out_specs=whole(rows, width),
@@ -321,7 +337,7 @@
         name="rest",
     )(
         offsets, valid_tiles, x, xp, gain, w_t, proj, proj, proj, own, jnp.asarray(local),
-        *mids, *mids, far_all, jnp.asarray(extra), sub_gain.reshape(width, 1), w_out,
+        *mids, *mids, far_key, far_value, jnp.asarray(extra), sub_gain.reshape(width, 1), w_out,
     )
     return (
         out.reshape(4, 4, groups, each, width).transpose(3, 2, 1, 0, 4).reshape(rows, width)

time: 137 us -> 115 us (0.84)
  waiting for transfers between devices: 54.4 us -> 30.4 us
  between operations: 14.1 us -> 0.8 us
  starting transfers between devices: 11.9 us -> 24.4 us
  local copies, waits for them, and re-layouts: 11.7 us -> 14.2 us
    all_gather x1 -> x0, waiting for transfers between devices: 30 us -> none  [body(): far_all = lax.all_gather(far, 'seq', axis=0, tiled=True)]
    ppermute x0 -> x8, waiting for transfers between devices: none -> 20 us  [doubled(): return jnp.concatenate([rows, lax.ppermute(rows, 'seq', pairs)], axis=0)]
    ppermute x0 -> x8, starting transfers between devices: none -> 12.8 us  [doubled(): return jnp.concatenate([rows, lax.ppermute(rows, 'seq', pairs)], axis=0)]
    ppermute x2, waiting for transfers between devices: 11.8 us -> 0.01 us  [body(): lax.ppermute(mid, 'seq', [(d, d ^ g) for d in range(devices)])]
    all_to_all x1, waiting for transfers between devices: 12.6 us -> 10.4 us  [body(): lax.all_to_all(pieces, 'seq', split_axis=0, concat_axis=0, tiled=True)]
    unnamed x11 -> x22, local copies, waits for them, and re-layouts: 5.78 us -> 7.43 us
  transfers between devices with their start and end apart: 5 -> 12, of which waited for: 3 -> 7; matrix products, arithmetic and copies ran while one was open for 6% -> 9% of each run, Pallas kernels for 8% -> 17%
where the time goes in v2:
time: 115 us; the launch traced here: 114 us
  Pallas kernels  44.1 us (38%)
  waiting for transfers between devices  30.4 us (26%)
  starting transfers between devices  24.4 us (21%)
  local copies, waits for them, and re-layouts  14.2 us (12%)
    pallas_call x1, Pallas kernels, body(): pl.pallas_call(functools.partial(rest_kernel, heads, scale, per_step, far...  25.2 us
    ppermute x8, waiting for transfers between devices, doubled(): return jnp.concatenate([rows, lax.ppermute(rows, 'seq', pairs)], axis=0)  20 us
    ppermute x8, starting transfers between devices, doubled(): return jnp.concatenate([rows, lax.ppermute(rows, 'seq', pairs)], axis=0)  12.8 us
    pallas_call x1, Pallas kernels, body(): pl.pallas_call(functools.partial(own_kernel, scale, per_step, size), grid...  10.7 us
    all_to_all x1, waiting for transfers between devices, body(): lax.all_to_all(pieces, 'seq', split_axis=0, concat_axis=0, tiled=True)  10.4 us
    all_to_all x1, starting transfers between devices, body(): lax.all_to_all(pieces, 'seq', split_axis=0, concat_axis=0, tiled=True)  8.34 us
    pallas_call x1, Pallas kernels, body(): pl.pallas_call(functools.partial(project_kernel, heads), out_shape=(jax.S...  8.2 us
    unnamed x22, local copies, waits for them, and re-layouts  7.43 us
  transfers between devices with their start and end apart: 12, of which 7 were waited for; matrix products, arithmetic and copies ran while one was open for 9% of the time, Pallas kernels for 17%

profile of v2, /device:TPU:0, one launch (start us, length us, event | category | flops | bytes accessed | tf_op | source)
XLA Modules:
  0.0 114.0 jit_solution(4675630125280895580)
XLA Ops:
  0.0 8.3 %all-to-all-start = ((bf16[16,32,768]{2,1,0:T(8,128)(2,1)}), bf16[16,32,768]{2,1,0:T(8,128)(2,1)S(1)}, u32[]{:S(2)}, u32[]{:S(2)}) async-start(bf16[16,32,768]{2,1,0:T(8,128)(2,1)} %bitcast.24), calls=%async_computation | async-start | bytes 1572864 | tf_op jit(solution)/shard_map/all_to_all | solution.py:243
  9.0 1.3 %reshape.30.gain_ref = f32[1,768]{1,0:T(1,128)} reshape(f32[768]{0:T(1024)} %param.12) | data formatting | bytes 6144 | tf_op jit(solution)/shard_map/reshape | solution.py:250
  10.3 1.6 %reshape.36.rest_7_ = f32[768,1]{1,0:T(8,128)} reshape(f32[768]{0:T(1024)} %param.14) | data formatting | bytes 6144 | tf_op jit(solution)/shard_map/reshape | solution.py:340
  11.9 5.8 %copy.14 = bf16[768,2304]{0,1:T(8,128)(2,1)} copy(bf16[768,2304]{1,0:T(8,128)(2,1)} %param.13) | data formatting | bytes 7077888 | tf_op args[4]
  17.6 10.4 %all-to-all-done = bf16[16,32,768]{2,1,0:T(8,128)(2,1)S(1)} async-done(((bf16[16,32,768]{2,1,0:T(8,128)(2,1)}), bf16[16,32,768]{2,1,0:T(8,128)(2,1)S(1)}, u32[]{:S(2)}, u32[]{:S(2)}) %all-to-all-start) | async-done | bytes 786464 | tf_op jit(solution)/shard_map/all_to_all | solution.py:243
  29.0 8.2 %project.1 = (bf16[2304,512]{1,0:T(8,128)(2,1)}, bf16[1536,128]{1,0:T(8,128)(2,1)}, bf16[32,768]{1,0:T(8,128)(2,1)}, bf16[32,768]{1,0:T(8,128)(2,1)}) custom-call(s32[16]{0:T(128)} %offs.3, bf16[512,768]{1,0:T(8,128)(2,1)} %bitcast.18, f32[1,768]{1,0:T(1,128)} %reshape.30.gain_ref, bf16[2304,768]{1,0:T(8,128)(2,1)} %bitcast.15), custom_call_target="tpu_custom_call" | custom-call | flops 1811939328 | bytes 7077888 | tf_op jit(solution)/shard_map/project/pallas_call | solution.py:252
  37.2 2.3 %collective-permute-start.2 = (bf16[1536,128]{1,0:T(8,128)(2,1)}, bf16[1536,128]{1,0:T(8,128)(2,1)S(1)}, u32[]{:S(2)}, u32[]{:S(2)}) collective-permute-start(bf16[1536,128]{1,0:T(8,128)(2,1)} %get-tuple-element.10), channel_id=1, source_target_pairs={{0,6},{2,4},{4,2},{6,0},{8,14},{10,12},{12,10},{14,8},{16,22},{18,... | collective-permute-start | bytes 1179656 | tf_op jit(solution)/shard_map/ppermute | solution.py:271
  39.9 0.8 collective-permute-start.3
  40.7 2.4 %collective-permute-start.7 = (bf16[32,768]{1,0:T(8,128)(2,1)}, bf16[32,768]{1,0:T(8,128)(2,1)S(1)}, u32[]{:S(2)}, u32[]{:S(2)}) collective-permute-start(bf16[32,768]{1,0:T(8,128)(2,1)} %get-tuple-element.12), channel_id=1, source_target_pairs={{0,16},{2,18},{4,20},{6,22},{8,24},{10,26},{12,28},{14,30},{16,0},... | collective-permute-start | bytes 147464 | tf_op jit(solution)/shard_map/ppermute | solution.py:223
  43.1 10.7 %own_keys.1.own_ref = f32[1024,512]{1,0:T(8,128)} custom-call(s32[1]{0:T(128)S(6)} %copy.26.valid, bf16[2304,512]{1,0:T(8,128)(2,1)} %get-tuple-element.9.q_ref.k_ref.v_ref, bf16[2304,512]{1,0:T(8,128)(2,1)} %get-tuple-element.9.q_ref.k_ref.v_ref, bf16[2304,512]{1,0:T(8,128)(2,1)} %get-tuple-element.9.q_ref.k_ref.v_ref, s32[1,512]{1,0:T(1,128)} %constant.4.clone.pos_ref.ppos_ref), custom_call_target="tpu_custom_call" | custom-call | flops 3221225472 | bytes 3145728 | tf_op jit(solution)/shard_map/own_keys/pallas_call | solution.py:296
  54.5 2.2 %collective-permute-start.4 = (bf16[64,768]{1,0:T(8,128)(2,1)S(1)}, bf16[64,768]{1,0:T(8,128)(2,1)S(1)}, u32[]{:S(2)}, u32[]{:S(2)}) collective-permute-start(bf16[64,768]{1,0:T(8,128)(2,1)S(1)} %pad_maximum_fusion.4), channel_id=1, source_target_pairs={{0,4},{2,6},{4,0},{6,2},{8,12},{10,14},{12,8},{14,10},{16,20},{18,... | collective-permute-start | bytes 294920 | tf_op jit(solution)/shard_map/ppermute | solution.py:223
  56.7 2.7 %collective-permute-start.8 = (bf16[64,768]{1,0:T(8,128)(2,1)S(1)}, bf16[64,768]{1,0:T(8,128)(2,1)S(1)}, u32[]{:S(2)}, u32[]{:S(2)}) collective-permute-start(bf16[64,768]{1,0:T(8,128)(2,1)S(1)} %pad_maximum_fusion.5), channel_id=1, source_target_pairs={{0,8},{2,10},{4,12},{6,14},{8,0},{10,2},{12,4},{14,6},{16,24},{18,... | collective-permute-start | bytes 294920 | tf_op jit(solution)/shard_map/ppermute | solution.py:223
  59.4 2.8 %collective-permute-done.8 = bf16[64,768]{1,0:T(8,128)(2,1)S(1)} collective-permute-done((bf16[64,768]{1,0:T(8,128)(2,1)S(1)}, bf16[64,768]{1,0:T(8,128)(2,1)S(1)}, u32[]{:S(2)}, u32[]{:S(2)}) %collective-permute-start.8) | collective-permute-done | bytes 98336 | tf_op jit(solution)/shard_map/ppermute | solution.py:223
  62.5 2.4 %collective-permute-start.5 = (bf16[128,768]{1,0:T(8,128)(2,1)S(1)}, bf16[128,768]{1,0:T(8,128)(2,1)S(1)}, u32[]{:S(2)}, u32[]{:S(2)}) collective-permute-start(bf16[128,768]{1,0:T(8,128)(2,1)S(1)} %pad_maximum_fusion.2), channel_id=1, source_target_pairs={{0,8},{2,10},{4,12},{6,14},{8,0},{10,2},{12,4},{14,6},{16,24},{18,... | collective-permute-start | bytes 589832 | tf_op jit(solution)/shard_map/ppermute | solution.py:223
  64.9 3.1 %collective-permute-done.9 = bf16[128,768]{1,0:T(8,128)(2,1)S(1)} collective-permute-done((bf16[128,768]{1,0:T(8,128)(2,1)S(1)}, bf16[128,768]{1,0:T(8,128)(2,1)S(1)}, u32[]{:S(2)}, u32[]{:S(2)}) %collective-permute-start.9) | collective-permute-done | bytes 196640 | tf_op jit(solution)/shard_map/ppermute | solution.py:223
  68.5 2.1 %collective-permute-done.5 = bf16[128,768]{1,0:T(8,128)(2,1)S(1)} collective-permute-done((bf16[128,768]{1,0:T(8,128)(2,1)S(1)}, bf16[128,768]{1,0:T(8,128)(2,1)S(1)}, u32[]{:S(2)}, u32[]{:S(2)}) %collective-permute-start.5) | collective-permute-done | bytes 196640 | tf_op jit(solution)/shard_map/ppermute | solution.py:223
  70.6 1.4 %collective-permute-start.6 = (bf16[256,768]{1,0:T(8,128)(2,1)S(1)}, bf16[256,768]{1,0:T(8,128)(2,1)S(1)}, u32[]{:S(2)}, u32[]{:S(2)}) collective-permute-start(bf16[256,768]{1,0:T(8,128)(2,1)S(1)} %pad_maximum_fusion), channel_id=1, source_target_pairs={{0,16},{2,18},{4,20},{6,22},{8,24},{10,26},{12,28},{14,30},{16,0},... | collective-permute-start | bytes 1179656 | tf_op jit(solution)/shard_map/ppermute | solution.py:223
  72.1 3.7 %collective-permute-done.10 = bf16[256,768]{1,0:T(8,128)(2,1)S(1)} collective-permute-done((bf16[256,768]{1,0:T(8,128)(2,1)S(1)}, bf16[256,768]{1,0:T(8,128)(2,1)S(1)}, u32[]{:S(2)}, u32[]{:S(2)}) %collective-permute-start.10) | collective-permute-done | bytes 393248 | tf_op jit(solution)/shard_map/ppermute | solution.py:223
  75.9 1.0 copy.15
  76.8 7.7 %collective-permute-done.6 = bf16[256,768]{1,0:T(8,128)(2,1)S(1)} collective-permute-done((bf16[256,768]{1,0:T(8,128)(2,1)S(1)}, bf16[256,768]{1,0:T(8,128)(2,1)S(1)}, u32[]{:S(2)}, u32[]{:S(2)}) %collective-permute-start.6) | collective-permute-done | bytes 393248 | tf_op jit(solution)/shard_map/ppermute | solution.py:223
  84.7 0.9 copy-done.3
  86.0 25.2 %rest.1 = bf16[512,768]{1,0:T(8,128)(2,1)} custom-call(s32[16]{0:T(128)} %offs.3, s32[1]{0:T(128)S(6)} %copy.26.valid, bf16[512,768]{1,0:T(8,128)(2,1)} %bitcast.19, bf16[512,768]{1,0:T(8,128)(2,1)} %copy-done.4, f32[1,768]{1,0:T(1,128)} %reshape.30.gain_ref, bf16[2304,768]{1,0:T(8,128)(2,1)} %bitcast.16, ...), custom_call_target="tpu_custom_call" | custom-call | flops 4831838208 | bytes 7864320 | tf_op jit(solution)/shard_map/rest/pallas_call | solution.py:310
  111.2 1.7 %copy.17 = bf16[32,1,4,4,768]{4,3,2,0,1:T(4,128)(2,1)S(1)} copy(bf16[32,1,4,4,768]{4,0,2,3,1:T(8,128)(2,1)} %bitcast.21) | data formatting | bytes 1572864 | tf_op jit(solution)/shard_map/transpose | solution.py:343
  113.0 1.1 reshape.35
  (39 shorter events, 3.4 us)
Async XLA Ops:
  0.0 28.0 %all-to-all-start = ((bf16[16,32,768]{2,1,0:T(8,128)(2,1)}), bf16[16,32,768]{2,1,0:T(8,128)(2,1)S(1)}, u32[]{:S(2)}, u32[]{:S(2)}) async-start(bf16[16,32,768]{2,1,0:T(8,128)(2,1)} %bitcast.24), calls=%async_computation | async-start | bytes 1572864 | tf_op jit(solution)/shard_map/all_to_all | solution.py:243
  28.1 0.9 copy-start
  28.1 56.6 %collective-permute-start = (bf16[512,768]{1,0:T(8,128)(2,1)S(1)}, bf16[512,768]{1,0:T(8,128)(2,1)S(1)}, u32[]{:S(2)}, u32[]{:S(2)}) collective-permute-start(bf16[512,768]{1,0:T(8,128)(2,1)S(1)} %bitcast.17), channel_id=1, source_target_pairs={{0,2},{2,0},{4,6},{6,4},{8,10},{10,8},{12,14},{14,12},{16,18},{18,... | collective-permute-start | bytes 2359304 | tf_op jit(solution)/shard_map/ppermute | solution.py:246
  37.2 47.5 %collective-permute-start.2 = (bf16[1536,128]{1,0:T(8,128)(2,1)}, bf16[1536,128]{1,0:T(8,128)(2,1)S(1)}, u32[]{:S(2)}, u32[]{:S(2)}) collective-permute-start(bf16[1536,128]{1,0:T(8,128)(2,1)} %get-tuple-element.10), channel_id=1, source_target_pairs={{0,6},{2,4},{4,2},{6,0},{8,14},{10,12},{12,10},{14,8},{16,22},{18,... | collective-permute-start | bytes 1179656 | tf_op jit(solution)/shard_map/ppermute | solution.py:271
  39.5 45.2 %collective-permute-start.1 = (bf16[1536,128]{1,0:T(8,128)(2,1)}, bf16[1536,128]{1,0:T(8,128)(2,1)S(1)}, u32[]{:S(2)}, u32[]{:S(2)}) collective-permute-start(bf16[1536,128]{1,0:T(8,128)(2,1)} %get-tuple-element.10), channel_id=1, source_target_pairs={{0,4},{2,6},{4,0},{6,2},{8,12},{10,14},{12,8},{14,10},{16,20},{18,... | collective-permute-start | bytes 1179656 | tf_op jit(solution)/shard_map/ppermute | solution.py:271
  39.9 14.6 %collective-permute-start.3 = (bf16[32,768]{1,0:T(8,128)(2,1)}, bf16[32,768]{1,0:T(8,128)(2,1)S(1)}, u32[]{:S(2)}, u32[]{:S(2)}) collective-permute-start(bf16[32,768]{1,0:T(8,128)(2,1)} %get-tuple-element.11), channel_id=1, source_target_pairs={{0,2},{2,0},{4,6},{6,4},{8,10},{10,8},{12,14},{14,12},{16,18},{18,... | collective-permute-start | bytes 147464 | tf_op jit(solution)/shard_map/ppermute | solution.py:223
  40.7 16.0 %collective-permute-start.7 = (bf16[32,768]{1,0:T(8,128)(2,1)}, bf16[32,768]{1,0:T(8,128)(2,1)S(1)}, u32[]{:S(2)}, u32[]{:S(2)}) collective-permute-start(bf16[32,768]{1,0:T(8,128)(2,1)} %get-tuple-element.12), channel_id=1, source_target_pairs={{0,16},{2,18},{4,20},{6,22},{8,24},{10,26},{12,28},{14,30},{16,0},... | collective-permute-start | bytes 147464 | tf_op jit(solution)/shard_map/ppermute | solution.py:223
  43.1 10.7 %copy-start.5 = (bf16[32,768]{1,0:T(8,128)(2,1)S(1)}, bf16[32,768]{1,0:T(8,128)(2,1)}, u32[]{:S(2)}) copy-start(bf16[32,768]{1,0:T(8,128)(2,1)} %get-tuple-element.11) | copy-start | bytes 147460
  43.1 10.7 %copy-start.6 = (bf16[32,768]{1,0:T(8,128)(2,1)S(1)}, bf16[32,768]{1,0:T(8,128)(2,1)}, u32[]{:S(2)}) copy-start(bf16[32,768]{1,0:T(8,128)(2,1)} %get-tuple-element.12) | copy-start | bytes 147460
  54.5 8.0 %collective-permute-start.4 = (bf16[64,768]{1,0:T(8,128)(2,1)S(1)}, bf16[64,768]{1,0:T(8,128)(2,1)S(1)}, u32[]{:S(2)}, u32[]{:S(2)}) collective-permute-start(bf16[64,768]{1,0:T(8,128)(2,1)S(1)} %pad_maximum_fusion.4), channel_id=1, source_target_pairs={{0,4},{2,6},{4,0},{6,2},{8,12},{10,14},{12,8},{14,10},{16,20},{18,... | collective-permute-start | bytes 294920 | tf_op jit(solution)/shard_map/ppermute | solution.py:223
  56.7 5.5 %collective-permute-start.8 = (bf16[64,768]{1,0:T(8,128)(2,1)S(1)}, bf16[64,768]{1,0:T(8,128)(2,1)S(1)}, u32[]{:S(2)}, u32[]{:S(2)}) collective-permute-start(bf16[64,768]{1,0:T(8,128)(2,1)S(1)} %pad_maximum_fusion.5), channel_id=1, source_target_pairs={{0,8},{2,10},{4,12},{6,14},{8,0},{10,2},{12,4},{14,6},{16,24},{18,... | collective-permute-start | bytes 294920 | tf_op jit(solution)/shard_map/ppermute | solution.py:223
  62.2 5.7 %collective-permute-start.9 = (bf16[128,768]{1,0:T(8,128)(2,1)S(1)}, bf16[128,768]{1,0:T(8,128)(2,1)S(1)}, u32[]{:S(2)}, u32[]{:S(2)}) collective-permute-start(bf16[128,768]{1,0:T(8,128)(2,1)S(1)} %pad_maximum_fusion.3), channel_id=1, source_target_pairs={{0,4},{2,6},{4,0},{6,2},{8,12},{10,14},{12,8},{14,10},{16,20},{18,... | collective-permute-start | bytes 589832 | tf_op jit(solution)/shard_map/ppermute | solution.py:223
  62.5 8.1 %collective-permute-start.5 = (bf16[128,768]{1,0:T(8,128)(2,1)S(1)}, bf16[128,768]{1,0:T(8,128)(2,1)S(1)}, u32[]{:S(2)}, u32[]{:S(2)}) collective-permute-start(bf16[128,768]{1,0:T(8,128)(2,1)S(1)} %pad_maximum_fusion.2), channel_id=1, source_target_pairs={{0,8},{2,10},{4,12},{6,14},{8,0},{10,2},{12,4},{14,6},{16,24},{18,... | collective-permute-start | bytes 589832 | tf_op jit(solution)/shard_map/ppermute | solution.py:223
  68.0 7.8 %collective-permute-start.10 = (bf16[256,768]{1,0:T(8,128)(2,1)S(1)}, bf16[256,768]{1,0:T(8,128)(2,1)S(1)}, u32[]{:S(2)}, u32[]{:S(2)}) collective-permute-start(bf16[256,768]{1,0:T(8,128)(2,1)S(1)} %pad_maximum_fusion.1), channel_id=1, source_target_pairs={{0,2},{2,0},{4,6},{6,4},{8,10},{10,8},{12,14},{14,12},{16,18},{18,... | collective-permute-start | bytes 1179656 | tf_op jit(solution)/shard_map/ppermute | solution.py:223
  70.6 14.0 %collective-permute-start.6 = (bf16[256,768]{1,0:T(8,128)(2,1)S(1)}, bf16[256,768]{1,0:T(8,128)(2,1)S(1)}, u32[]{:S(2)}, u32[]{:S(2)}) collective-permute-start(bf16[256,768]{1,0:T(8,128)(2,1)S(1)} %pad_maximum_fusion), channel_id=1, source_target_pairs={{0,16},{2,18},{4,20},{6,22},{8,24},{10,26},{12,28},{14,30},{16,0},... | collective-permute-start | bytes 1179656 | tf_op jit(solution)/shard_map/ppermute | solution.py:223
  84.6 0.9 copy-start.3
  84.6 1.0 copy-start.1
  84.7 1.2 %copy-start.2 = (bf16[1536,128]{1,0:T(8,128)(2,1)}, bf16[1536,128]{1,0:T(8,128)(2,1)S(1)}, u32[]{:S(2)}) copy-start(bf16[1536,128]{1,0:T(8,128)(2,1)S(1)} %collective-permute-done.1.rest_0_.rest_2_) | copy-start | bytes 1179652
  84.7 1.4 %copy-start.4 = (bf16[512,768]{1,0:T(8,128)(2,1)}, bf16[512,768]{1,0:T(8,128)(2,1)S(1)}, u32[]{:S(2)}) copy-start(bf16[512,768]{1,0:T(8,128)(2,1)S(1)} %collective-permute-done.xp_ref) | copy-start | bytes 2359300
